TPU v7x, 512 devices: a 4x2x32 block of a 4x8x32 slice. The times are simulated.
512 devices in a mesh: parts: 2 (over y), seq: 32 (over z), tp: 8 (over x, core).
Axes of the slice: x: 4, y: 2, z: 32, core: 2. Of those that a mesh axis runs over, the one named last changes fastest.
The devices are a block of a 4x8x32 slice.
Arguments:
- tokens: bfloat16 [16384, 8192], P(('parts', 'seq'), 'tp'), parts along dimension 0, may hold values from -6 to 6
- norm_gain: bfloat16 [8192], P('tp'), may hold values from 0.099609375 to 1.8984375
- w_query: bfloat16 [8192, 4096], P('seq', 'tp'), may hold values from -0.0625 to 0.0625
- w_kv: bfloat16 [8192, 2, 1024], P('seq', None, 'tp'), may hold values from -0.0625 to 0.0625
- b_query: float32 [4096], P('tp'), may hold values from -4 to 4
- b_kv: float32 [2, 1024], P(None, 'tp'), may hold values from -4 to 4
- kv_pool: bfloat16 [8192, 2, 8, 1024], P(('parts', 'seq'), None, None, 'tp'), parts along dimension 0, may hold values from -68 to 68
- prefix_pages: int32 [128, 32], P('parts'), parts along dimension 0, may hold values from 0 to 4095, as said below
- prefix_len: int32 [128], P('parts'), parts along dimension 0, may hold values from 0 to 256
- suffix_len: int32 [128], P('parts'), parts along dimension 0, may hold values from 1 to 128
- fresh_owner: int32 [2048, 1], P('parts'), parts along dimension 0, may hold values from 0 to 31; in each aligned block of 32 rows (0 to 31, 32 to 63, ...) at most 2 rows name the same one
Outputs:
- attn_out: bfloat16 [16384, 4096], P(('parts', 'seq'), 'tp'), parts along dimension 0
- fresh_pages: bfloat16 [4096, 2, 8, 1024], P(('parts', 'seq'), None, None, 'tp'), parts along dimension 0
There are 2 independent parts, one for each index of `parts`. A program takes and returns all parts, laid end to end along the dimension named above; an argument that names none is the same for every part. Nothing has to cross between parts.
Inputs may be any that keep to these rules, and one draw needn't show every extreme that they name: `prefix_pages`: page id q lies in the 128 pages of sequence group q // 128. Among the 64 entries of requests 2*g to 2*(g+1)-1, no group holds more than 3, and in every such block some group holds exactly 3. Entries past the matched prefix still name pages. `fresh_owner`: in the rows of one sequence group's requests (aligned blocks of 32 rows) no group is named more than 2 times; some blocks name one exactly 2 times.
All inputs are finite; a program needn't handle non-finite values.
Results may differ from a plain program's by a relative error of at most 0.005.
The roundings to bfloat16 on the way count: a program that leaves them out, or rounds other values in their place, can miss the bound.
Values may be sent and summed in bfloat16 or wider, within the bound.
A program may use at most 64 MiB of HBM per device.

v0:
```python
import math

import jax
import jax.numpy as jnp
from jax import lax
from jax.sharding import PartitionSpec as P

HEAD_DIM = 128
BLOCK = 128
PAGE = 8


def rows_first(arrays, axis, dims):
    turned = [jnp.moveaxis(a, dim, 0) for a, dim in zip(arrays, dims)]
    widths = [t[0].size for t in turned]
    both = jnp.concatenate([t.reshape(-1, w) for t, w in zip(turned, widths)], axis=1)
    result = lax.all_gather(both, axis, axis=0, tiled=True)
    tiles = jnp.split(result, [sum(widths[:k]) for k in range(1, len(widths))], axis=1)
    return tuple(
        (
            jnp.moveaxis(b.reshape(-1, *t.shape[1:]), 0, dim)
            for b, t, dim in zip(tiles, turned, dims)
        )
    )


def in_one_piece(arrays, axis, dim, along):
    columns = [a.reshape(*a.shape[:along], -1) for a in arrays]
    both = jnp.concatenate(columns, axis=along)
    result, at, gathered = (lax.all_gather(both, axis, axis=dim, tiled=True), 0, [])
    for a, column in zip(arrays, columns):
        section = result[..., at : at + column.shape[along]]
        gathered.append(section.reshape(*section.shape[:along], *a.shape[along:]))
        at += column.shape[along]
    return tuple(gathered)


def rotate(values, positions):
    half_dim = values.shape[-1] // 2
    freq_index = jnp.arange(half_dim, dtype=jnp.float32)
    inverse = jnp.exp(freq_index * (-2.0 * math.log(1000000.0) / values.shape[-1]))
    angles = positions.astype(jnp.float32)[..., None, None] * inverse
    cosine = jnp.cos(angles)
    sine = jnp.sin(angles)
    first_half = values[..., :half_dim]
    second_half = values[..., half_dim:]
    return jnp.concatenate(
        [first_half * cosine - second_half * sine, second_half * cosine + first_half * sine],
        axis=-1,
    )


def attend(query, key_new, value_new, key_old, value_old, prefix_mine, suffix_mine):
    batch, block_len, heads_here, head_dim = query.shape
    kv_here = key_new.shape[2]
    group_size = heads_here // kv_here
    old_len = key_old.shape[1]
    grouped = query.reshape(batch, block_len, kv_here, group_size, head_dim)
    all_keys = jnp.concatenate([key_old, key_new], axis=1)
    all_values = jnp.concatenate([value_old, value_new], axis=1)
    scores = jnp.einsum(
        "btkgd,bskd->bkgts", grouped, all_keys, preferred_element_type=jnp.float32
    ) / math.sqrt(head_dim)
    key_pos = jnp.arange(old_len + block_len, dtype=jnp.int32)
    query_pos = jnp.arange(block_len, dtype=jnp.int32)
    in_prefix = key_pos[None, None, :] < prefix_mine[:, None, None]
    shifted = key_pos - old_len
    in_suffix = (shifted[None, None, :] <= query_pos[None, :, None]) & (
        shifted[None, None, :] < suffix_mine[:, None, None]
    )
    allowed = jnp.where(key_pos[None, None, :] < old_len, in_prefix, in_suffix)[:, None, None]
    masked = jnp.where(allowed, scores, -1e30)
    peak = jnp.max(masked, axis=-1, keepdims=True)
    weights = jnp.where(allowed, jnp.exp(masked - peak), 0.0)
    probs = (weights / jnp.sum(weights, axis=-1, keepdims=True)).astype(jnp.bfloat16)
    mixed = jnp.einsum("bkgts,bskd->btkgd", probs, all_values, preferred_element_type=jnp.float32)
    live = query_pos[None, :] < suffix_mine[:, None]
    mixed = jnp.where(live[:, :, None, None, None], mixed, 0.0)
    return mixed.reshape(batch * block_len, heads_here * head_dim).astype(jnp.bfloat16)


def body(
    tokens,
    norm_gain,
    w_query,
    w_kv,
    b_query,
    b_kv,
    kv_pool,
    prefix_pages,
    prefix_len,
    suffix_len,
    fresh_owner,
):
    seq_count = lax.axis_size("seq")
    my_group = lax.axis_index("seq")
    token_rows = tokens.shape[0]
    blocks_here = token_rows // BLOCK
    kv_width = w_kv.shape[2]
    kv_here = kv_width // HEAD_DIM
    query_width = w_query.shape[1]
    heads_here = query_width // HEAD_DIM
    pool_pages = kv_pool.shape[0]
    page_slots = prefix_pages.shape[1]
    prefix_entries = blocks_here * page_slots
    suffix_pages = BLOCK // PAGE
    fresh_entries = blocks_here * suffix_pages
    prefix_cap = max(3, prefix_entries // seq_count + 1)
    fresh_cap = max(2, (fresh_entries + seq_count - 1) // seq_count + 1)
    first_row = my_group * blocks_here
    prefix_mine = lax.dynamic_slice_in_dim(prefix_len, first_row, blocks_here)
    suffix_mine = lax.dynamic_slice_in_dim(suffix_len, first_row, blocks_here)
    owners_mine = lax.dynamic_slice_in_dim(
        fresh_owner[:, 0], first_row * suffix_pages, fresh_entries
    )
    gathered, gain_whole = rows_first((tokens, norm_gain), "tp", (1, 0))
    widened = gathered.astype(jnp.float32)
    mean_square = jnp.mean(widened * widened, axis=-1, keepdims=True)
    normed = (widened * lax.rsqrt(mean_square + 1e-06) * gain_whole.astype(jnp.float32)).astype(
        jnp.bfloat16
    )
    all_ids = prefix_pages.reshape(seq_count, prefix_entries)
    all_owner = all_ids // pool_pages
    entry_ids = jnp.arange(prefix_entries, dtype=jnp.int32)
    before = (all_owner[:, :, None] == all_owner[:, None, :]) & (
        entry_ids[None, None, :] < entry_ids[None, :, None]
    )
    all_rank = jnp.sum(before.astype(jnp.int32), axis=-1)
    prefix_slots = jnp.arange(prefix_cap, dtype=jnp.int32)
    chosen = (all_owner[:, None, :] == my_group) & (
        all_rank[:, None, :] == prefix_slots[None, :, None]
    )
    picked = jnp.sum(jnp.where(chosen, entry_ids[None, None, :], 0), axis=-1)
    local_page = jnp.take_along_axis(all_ids, picked, axis=1) % pool_pages
    prefix_send = kv_pool[local_page]
    prefix_got = lax.all_to_all(prefix_send, "seq", split_axis=0, concat_axis=0, tiled=True)
    pieces = in_one_piece((w_query, w_kv), "seq", 0, 1)
    query_sums, pair_sums = tuple(
        (
            jnp.dot(
                normed,
                weight_piece.reshape(weight_piece.shape[0], -1),
                preferred_element_type=jnp.float32,
            )
            for weight_piece in pieces
        )
    )
    pair_lin = pair_sums + b_kv.reshape(1, 2 * kv_width)
    slot_ids = jnp.arange(BLOCK, dtype=jnp.int32)
    positions = prefix_mine[:, None] + slot_ids[None, :]
    live = (slot_ids[None, :] < suffix_mine[:, None])[:, :, None, None]
    key_new = jnp.where(
        live,
        rotate(pair_lin[:, :kv_width].reshape(blocks_here, BLOCK, kv_here, HEAD_DIM), positions),
        0.0,
    ).astype(jnp.bfloat16)
    value_new = jnp.where(
        live, pair_lin[:, kv_width:].reshape(blocks_here, BLOCK, kv_here, HEAD_DIM), 0.0
    ).astype(jnp.bfloat16)
    new_pages = jnp.stack(
        [
            key_new.reshape(fresh_entries, PAGE, kv_width),
            value_new.reshape(fresh_entries, PAGE, kv_width),
        ],
        axis=1,
    )
    fresh_ids = jnp.arange(fresh_entries, dtype=jnp.int32)
    fresh_before = (owners_mine[None, :] == owners_mine[:, None]) & (
        fresh_ids[None, :] < fresh_ids[:, None]
    )
    fresh_rank = jnp.sum(fresh_before.astype(jnp.int32), axis=1)
    group_ids = jnp.arange(seq_count, dtype=jnp.int32)
    fresh_slots = jnp.arange(fresh_cap, dtype=jnp.int32)
    placed = (owners_mine[None, None, :] == group_ids[:, None, None]) & (
        fresh_rank[None, None, :] == fresh_slots[None, :, None]
    )
    source = jnp.sum(jnp.where(placed, fresh_ids[None, None, :], 0), axis=-1)
    filled = jnp.any(placed, axis=-1)
    fresh_send = jnp.where(
        filled[:, :, None, None, None], new_pages[source], jnp.zeros((), jnp.bfloat16)
    )
    fresh_got = lax.all_to_all(fresh_send, "seq", split_axis=0, concat_axis=0, tiled=True)
    query_lin = query_sums + b_query[None, :]
    query = rotate(query_lin.reshape(blocks_here, BLOCK, heads_here, HEAD_DIM), positions).astype(
        jnp.bfloat16
    )
    my_rank = lax.dynamic_index_in_dim(all_rank, my_group, 0, keepdims=False)
    my_ids = lax.dynamic_index_in_dim(all_ids, my_group, 0, keepdims=False)
    arrived_at = my_ids // pool_pages * prefix_cap + my_rank
    fetched = prefix_got.reshape(seq_count * prefix_cap, 2, PAGE, kv_width)[arrived_at]
    fetched = fetched.reshape(blocks_here, page_slots, 2, PAGE, kv_here, HEAD_DIM)
    key_old = fetched[:, :, 0].reshape(blocks_here, page_slots * PAGE, kv_here, HEAD_DIM)
    value_old = fetched[:, :, 1].reshape(blocks_here, page_slots * PAGE, kv_here, HEAD_DIM)
    attn_out = attend(query, key_new, value_new, key_old, value_old, prefix_mine, suffix_mine)
    fresh_out = fresh_got.reshape(seq_count * fresh_cap, 2, PAGE, kv_width)
    return (attn_out, fresh_out)


def solution(mesh):
    placed = (
        P(("parts", "seq"), "tp"),
        P("tp"),
        P("seq", "tp"),
        P("seq", None, "tp"),
        P("tp"),
        P(None, "tp"),
        P(("parts", "seq"), None, None, "tp"),
        P("parts", None),
        P("parts"),
        P("parts"),
        P("parts", None),
    )
    return jax.shard_map(
        body,
        mesh=mesh,
        in_specs=placed,
        out_specs=(P(("parts", "seq"), "tp"), P(("parts", "seq"), None, None, "tp")),
        check_vma=False,
    )
```

profile of v0, /device:TPU:40, one launch (start us, length us, event | category | flops | bytes accessed | tf_op | source)
XLA Modules:
  0.0 323.2 jit_solution(4493974345548147127)
XLA Ops:
  7.3 0.7 reshape.693
  8.0 1.9 pad_maximum_fusion
  10.0 0.9 copy.65
  10.9 1.7 pad_maximum_fusion.1
  12.7 0.8 copy.35
  13.6 0.9 convert_reduce_fusion
  15.0 1.3 gather_fusion.3
  16.7 1.4 gather_fusion
  18.1 45.8 %all-to-all-start = ((bf16[32,3,2,8,128]{4,3,2,1,0:T(8,128)(2,1)}), bf16[32,3,2,8,128]{4,3,2,1,0:T(8,128)(2,1)S(1)}, u32[]{:S(2)}, u32[]{:S(2)}) async-start(bf16[32,3,2,8,128]{4,3,2,1,0:T(8,128)(2,1)} %bitcast.1), calls=%async_computation | async-start | bytes 786432 | tf_op jit(solution)/shard_map/all_to_all | solution.py:136
  63.9 0.7 fusion.46
  66.2 0.3 and_select_fusion
  66.5 0.5 multiply_cosine_fusion
  67.1 50.0 %all-to-all-done = bf16[32,3,2,8,128]{4,3,2,1,0:T(8,128)(2,1)S(1)} async-done(((bf16[32,3,2,8,128]{4,3,2,1,0:T(8,128)(2,1)}), bf16[32,3,2,8,128]{4,3,2,1,0:T(8,128)(2,1)S(1)}, u32[]{:S(2)}, u32[]{:S(2)}) %all-to-all-start) | async-done | bytes 393248 | tf_op jit(solution)/shard_map/all_to_all | solution.py:136
  117.0 0.6 gather_fusion.1
  117.9 3.2 fusion
  121.0 0.9 slice_convert_fusion
  122.0 129.2 %all-gather.5.cloned.1.call-done = bf16[8192,768]{1,0:T(8,128)(2,1)} async-done(((bf16[256,768]{1,0:T(8,128)(2,1)}), bf16[8192,768]{1,0:T(8,128)(2,1)}) %all-gather.5.cloned.1.call-update) | async-done | bytes 12582928 | tf_op jit(solution)/shard_map/all_gather | solution.py:30
  251.2 4.8 %fusion.14 = f32[256,256]{1,0:T(8,128)S(1)} fusion(bf16[8192,768]{1,0:T(8,128)(2,1)} %all-gather.5.cloned.1.call-done, f32[8192]{0:T(1024)S(1)} %bitcast.112, f32[256]{0:T(256)S(1)} %add_rsqrt_fusion, bf16[8192,257]{0,1:T(8,128)(2,1)} %all-gather.3.cloned.1.call-done, f32[256]{0:T(256)S(1)} %bitcast.114), kind=kOutput, calls=%fused_computation.22 | convolution fusion | flops 1082195968 | bytes 8685568 | tf_op jit(solution)/shard_map/dot_general | solution.py:140
  256.0 0.6 fusion.32
  256.8 0.7 gather_fusion.2
  257.4 0.8 broadcast_select_fusion
  258.3 16.0 %all-to-all-start.1 = ((bf16[32,2,2,8,128]{4,3,2,1,0:T(8,128)(2,1)}), bf16[32,2,2,8,128]{4,3,2,1,0:T(8,128)(2,1)S(1)}, u32[]{:S(2)}, u32[]{:S(2)}) async-start(bf16[32,2,2,8,128]{4,3,2,1,0:T(8,128)(2,1)} %broadcast_select_fusion), calls=%async_computation.1 | async-start | bytes 524288 | tf_op jit(solution)/shard_map/all_to_all | solution.py:182
  274.3 7.0 %fusion.8 = f32[256,512]{1,0:T(8,128)S(1)} fusion(bf16[8192,768]{1,0:T(8,128)(2,1)} %all-gather.5.cloned.1.call-done, f32[8192]{0:T(1024)S(1)} %bitcast.113, f32[256]{0:T(256)S(1)} %add_rsqrt_fusion, bf16[8192,257]{0,1:T(8,128)(2,1)} %all-gather.3.cloned.1.call-done, f32[512]{0:T(512)S(1)} %copy-done.1), kind=kOutput, calls=%fused_computation.18 | convolution fusion | flops 2156003328 | bytes 13143040 | tf_op jit(solution)/shard_map/dot_general | solution.py:140
  281.4 0.2 reshape.699
  281.8 0.3 fusion.51
  282.3 0.5 fusion.52
  282.8 0.3 fusion.7
  283.1 0.5 fusion.13
  283.6 0.2 copy.46
  283.8 0.7 copy.64
  284.6 31.1 %all-to-all-done.1 = bf16[32,2,2,8,128]{4,3,2,1,0:T(8,128)(2,1)S(1)} async-done(((bf16[32,2,2,8,128]{4,3,2,1,0:T(8,128)(2,1)}), bf16[32,2,2,8,128]{4,3,2,1,0:T(8,128)(2,1)S(1)}, u32[]{:S(2)}, u32[]{:S(2)}) %all-to-all-start.1) | async-done | bytes 262176 | tf_op jit(solution)/shard_map/all_to_all | solution.py:182
  315.6 0.7 copy.67
  (63 shorter events, 3.4 us)
Async XLA Ops:
  7.2 9.5 %copy-start = (bf16[128,2,8,128]{3,2,1,0:T(8,128)(2,1)S(1)}, bf16[128,2,8,128]{3,2,1,0:T(8,128)(2,1)}, u32[]{:S(2)}) copy-start(bf16[128,2,8,128]{3,2,1,0:T(8,128)(2,1)} %param.17) | copy-start | bytes 1572868
  7.2 110.7 %all-gather.3.cloned.1.call-start = ((), (), s32[]{:S(2)}) async-start(), calls=%async_computation.2 | async-start | bytes 4866048 | tf_op jit(solution)/shard_map/all_gather | solution.py:17
  9.9 241.3 %all-gather.5.cloned.1.call-start = ((), (), s32[]{:S(2)}) async-start(), calls=%async_computation.3 | async-start | bytes 12976128 | tf_op jit(solution)/shard_map/all_gather | solution.py:30
  14.9 49.9 %copy-start.3 = (s32[64]{0:T(128)S(1)}, s32[64]{0:T(128)}, u32[]{:S(2)}) copy-start(s32[64]{0:T(128)} %param.19) | copy-start | bytes 772
  15.0 49.9 %copy-start.4 = (s32[64]{0:T(128)S(1)}, s32[64]{0:T(128)}, u32[]{:S(2)}) copy-start(s32[64]{0:T(128)} %param.20) | copy-start | bytes 772
  16.2 235.0 %copy-start.2 = (f32[2,128]{1,0:T(2,128)S(1)}, f32[2,128]{1,0:T(2,128)}, u32[]{:S(2)}) copy-start(f32[2,128]{1,0:T(2,128)} %param.16) | copy-start | bytes 3076
  18.1 98.9 %all-to-all-start = ((bf16[32,3,2,8,128]{4,3,2,1,0:T(8,128)(2,1)}), bf16[32,3,2,8,128]{4,3,2,1,0:T(8,128)(2,1)S(1)}, u32[]{:S(2)}, u32[]{:S(2)}) async-start(bf16[32,3,2,8,128]{4,3,2,1,0:T(8,128)(2,1)} %bitcast.1), calls=%async_computation | async-start | bytes 786432 | tf_op jit(solution)/shard_map/all_to_all | solution.py:136
  251.2 23.1 %copy-start.1 = (f32[512]{0:T(512)S(1)}, f32[512]{0:T(512)}, u32[]{:S(2)}) copy-start(f32[512]{0:T(512)} %param.15) | copy-start | bytes 6148
  258.3 57.4 %all-to-all-start.1 = ((bf16[32,2,2,8,128]{4,3,2,1,0:T(8,128)(2,1)}), bf16[32,2,2,8,128]{4,3,2,1,0:T(8,128)(2,1)S(1)}, u32[]{:S(2)}, u32[]{:S(2)}) async-start(bf16[32,2,2,8,128]{4,3,2,1,0:T(8,128)(2,1)} %broadcast_select_fusion), calls=%async_computation.1 | async-start | bytes 524288 | tf_op jit(solution)/shard_map/all_to_all | solution.py:182
Sparse Core Ops, SparseCore 0:
  10.2 72.8 all-gather.2
  85.2 165.9 all-gather.4
where the time goes:
time: 324 us; the launch traced here: 323 us
  waiting for transfers between devices  210 us (65%)
  starting transfers between devices  61.9 us (19%)
  between operations  14.4 us (4%)
  matrix products  12.8 us (4%)
  other arithmetic  12.7 us (4%)
  local copies, waits for them, and re-layouts  10.9 us (3%)
    all_gather x1, waiting for transfers between devices, in_one_piece(): lax.all_gather(both, axis, axis=dim, tiled=True)  129 us
    all_to_all x1, waiting for transfers between devices, body(): lax.all_to_all(prefix_send, 'seq', split_axis=0, concat_axis=0, tiled=True)  50 us
    all_to_all x1, starting transfers between devices, body(): lax.all_to_all(prefix_send, 'seq', split_axis=0, concat_axis=0, tiled=True)  45.8 us
    all_to_all x1, waiting for transfers between devices, body(): lax.all_to_all(fresh_send, 'seq', split_axis=0, concat_axis=0, tiled=True)  31.1 us
    all_to_all x1, starting transfers between devices, body(): lax.all_to_all(fresh_send, 'seq', split_axis=0, concat_axis=0, tiled=True)  16 us
    dot_general x2, matrix products, body(): jnp.dot(normed, weight_piece.reshape(weight_piece.shape[0], -1), preferre...  11.8 us
  transfers between devices with their start and end apart: 4, of which 3 were waited for; matrix products, arithmetic and copies ran while one was open for 8% of the time, Pallas kernels for 0%

commit v1 on v0

v1 whole, which is shorter than its diff:
```python
import functools
import math

import jax
import jax.numpy as jnp
from jax import lax
from jax.experimental import pallas as pl
from jax.experimental.pallas import tpu as pltpu
from jax.sharding import PartitionSpec as P

HEAD_DIM = 128
BLOCK = 128
PAGE = 8
MESH = pl.DeviceIdType.MESH

NORM_AT = 7
PREFIX_LAG = 12
CATCH_UP = 4


def offsets(count):
    starts, at = [], 0
    for step in range(1, count + 1):
        starts.append(at)
        at += count - step + 1
    return starts, at


class Ring:
    def __init__(self, make, steps):
        self.make, self.steps, self.started = make, steps, {}

    def start(self, step):
        if step > self.steps:
            return
        if step > 2:
            self.started.pop(step - 2).wait_send()
        copy = self.make(step)
        copy.start()
        self.started[step] = copy

    def arrive(self, step):
        if step <= self.steps:
            self.make(step).wait_recv()

    def drain(self):
        for copy in self.started.values():
            copy.wait_send()
        self.started = {}


def gather_kernel(
    n_parts, n_seq, n_tp,
    tok_ref, gain_ref, wkv_ref, wq_ref, bkv_ref, cos_ref, sin_ref, live_ref, psend_ref, source_ref,
    q0_ref, q1_ref, knew_ref, vnew_ref, got_ref, fresh_ref,
    toks, gains, nrm, wkvb, wqb0, wqb1, acc, pg_r, pg_l, fsend, fg_r, fg_l, newp,
    ring_send, ring_recv, y_send, y_recv, tok_send, tok_recv, gain_send, gain_recv,
):
    part, me, tp = lax.axis_index("parts"), lax.axis_index("seq"), lax.axis_index("tp")
    right, left = lax.rem(me + 1, n_seq), lax.rem(me + n_seq - 1, n_seq)
    up, down = lax.rem(part + 1, n_parts), lax.rem(part + n_parts - 1, n_parts)
    n_r, n_l = n_seq // 2, (n_seq - 1) // 2
    y_r, y_l = n_parts // 2, (n_parts - 1) // 2
    partner = tp + 1 - 2 * lax.rem(tp, 2)
    x_right, x_left = lax.rem(tp + 2, n_tp), lax.rem(tp + n_tp - 2, n_tp)
    x_far = lax.rem(tp + n_tp // 2, n_tp)
    rows = tok_ref.shape[0]
    half = rows // 2
    depth = wkv_ref.shape[0]
    features = tok_ref.shape[1]

    barrier = pltpu.get_barrier_semaphore()
    greeted = [{"seq": right}, {"seq": left}]
    greeted += [{"tp": lax.rem(tp + r, n_tp)} for r in range(1, n_tp)]
    if n_parts > 1:
        greeted.append({"parts": up})
    if n_parts > 2:
        greeted.append({"parts": down})
    for device in greeted:
        pl.semaphore_signal(barrier, inc=1, device_id=device, device_id_type=MESH)
    pl.semaphore_wait(barrier, len(greeted))

    def remote(src, dst, send, recv, device):
        return pltpu.make_async_remote_copy(
            src_ref=src, dst_ref=dst, send_sem=send, recv_sem=recv,
            device_id=device, device_id_type=MESH,
        )

    def slot(direction, step):
        return 2 * step - 1 if direction == 0 else 2 * step

    def ring(stream, direction, make_refs):
        target = {"seq": right if direction == 0 else left}

        def make(step):
            src, dst = make_refs(step)
            return remote(
                src, dst, ring_send.at[stream, direction, step % 2],
                ring_recv.at[stream, direction, step - 1], target,
            )

        return Ring(make, n_r if direction == 0 else n_l)

    def kv_refs(direction):
        def refs(step):
            src = wkv_ref if step == 1 else wkvb.at[slot(direction, step - 1)]
            return src, wkvb.at[slot(direction, step)]

        return refs

    q_cols = q0_ref.shape[1]

    def q_refs(direction, buffer, which):
        def refs(step):
            if step == 1:
                src = wq_ref.at[part, :, pl.ds(which * q_cols, q_cols)]
            else:
                src = buffer.at[slot(direction, step - 1), part]
            return src, buffer.at[slot(direction, step), part]

        return refs

    starts_r, _ = offsets(n_r)
    starts_l, _ = offsets(n_l)

    def block_refs(direction, first, buffer):
        count = n_r if direction == 0 else n_l
        starts = starts_r if direction == 0 else starts_l

        def refs(step):
            size = count - step + 1
            if step == 1:
                src = first.at[pl.ds(1 if direction == 0 else 1 + n_r, count)]
            else:
                src = buffer.at[pl.ds(starts[step - 2] + 1, size)]
            return src, buffer.at[pl.ds(starts[step - 1], size)]

        return refs

    kv = [ring(0, d, kv_refs(d)) for d in (0, 1)]
    q_ring = [
        [ring(1 + w, d, q_refs(d, buffer, w)) for d in (0, 1)]
        for w, buffer in enumerate((wqb0, wqb1))
    ]
    prefix = [ring(3, d, block_refs(d, psend_ref, (pg_r, pg_l)[d])) for d in (0, 1)]
    fresh = [ring(4, d, block_refs(d, fsend, (fg_r, fg_l)[d])) for d in (0, 1)]

    y_open = {}

    def y_make(which, step, direction, hop):
        buffer = (wqb0, wqb1)[which]
        origin = lax.rem(part + (n_parts - hop + 1 if direction == 0 else hop - 1), n_parts)
        pair = pl.ds(2 * step - 1, 2 if step <= n_l else 1)
        lane = hop - 1 if direction == 0 else y_r + hop - 1
        return remote(
            buffer.at[pair, origin], buffer.at[pair, origin],
            y_send.at[which, lane, step % 2], y_recv.at[which, lane, step - 1],
            {"parts": up if direction == 0 else down},
        )

    def y_start(which, step, direction, hop):
        if hop > (y_r if direction == 0 else y_l):
            return
        key = (which, direction, hop)
        if (key, step - 2) in y_open:
            y_open.pop((key, step - 2)).wait_send()
        copy = y_make(which, step, direction, hop)
        copy.start()
        y_open[(key, step)] = copy

    def y_arrive(which, step, direction, hop):
        if hop > (y_r if direction == 0 else y_l):
            return
        buffer = (wqb0, wqb1)[which]
        origin = lax.rem(part + (n_parts - hop if direction == 0 else hop), n_parts)
        pair = pl.ds(2 * step - 1, 2 if step <= n_l else 1)
        lane = hop - 1 if direction == 0 else y_r + hop - 1
        remote(
            buffer.at[pair, origin], buffer.at[pair, origin],
            y_send.at[which, lane, step % 2], y_recv.at[which, lane, step - 1],
            {"parts": up if direction == 0 else down},
        ).wait_recv()

    lo, hi = pl.ds(0, half), pl.ds(half, half)

    def tok_copy(index, src, block, part_rows, device):
        dst = toks.at[block] if part_rows is None else toks.at[block, part_rows]
        if src is None:
            src = dst
        return remote(src, dst, tok_send.at[index], tok_recv.at[index], {"tp": device})

    tok_open = []

    def tok_start(*args):
        copy = tok_copy(*args)
        copy.start()
        tok_open.append(copy)

    for d in (0, 1):
        kv[d].start(1)
        q_ring[0][d].start(1)
    tok_start(1, tok_ref, tp, None, x_right)
    tok_start(2, tok_ref, tp, None, x_left)
    tok_start(0, tok_ref, tp, None, partner)
    gain_open = []
    for r in range(1, n_tp):
        copy = remote(
            gain_ref, gains.at[tp], gain_send.at[r - 1], gain_recv.at[r - 1],
            {"tp": lax.rem(tp + r, n_tp)},
        )
        copy.start()
        gain_open.append(copy)
    toks[tp] = tok_ref[...]
    gains[tp] = gain_ref[...]
    acc[...] = jnp.zeros_like(acc)
    q0_ref[...] = jnp.zeros_like(q0_ref)
    q1_ref[...] = jnp.zeros_like(q1_ref)
    got_ref[0] = psend_ref[0]

    def tokens_near():
        tok_copy(1, None, x_left, None, x_right).wait_recv()
        tok_start(5, None, x_left, lo, x_right)
        tok_start(3, None, x_left, None, partner)
        tok_copy(2, None, x_right, None, x_left).wait_recv()
        tok_start(6, None, x_right, hi, x_left)
        tok_start(4, None, x_right, None, partner)

    def tokens_far():
        tok_copy(5, None, x_far, lo, x_right).wait_recv()
        tok_start(7, None, x_far, lo, partner)
        tok_copy(6, None, x_far, hi, x_left).wait_recv()
        tok_start(8, None, x_far, hi, partner)

    def shifted(base, by):
        return lax.rem(base + by, n_tp)

    def normalise():
        p_left, p_right = shifted(partner, n_tp - 2), shifted(partner, 2)
        p_far = shifted(partner, n_tp // 2)
        for index, block, part_rows in (
            (0, partner, None), (3, p_left, None), (4, p_right, None),
            (7, p_far, lo), (8, p_far, hi),
        ):
            tok_copy(index, None, block, part_rows, partner).wait_recv()
        for r in range(1, n_tp):
            remote(
                gain_ref, gains.at[lax.rem(tp + n_tp - r, n_tp)],
                gain_send.at[r - 1], gain_recv.at[r - 1], {"tp": lax.rem(tp + r, n_tp)},
            ).wait_recv()
        step_rows = 16

        def some_rows(i, carry):
            at = pl.ds(pl.multiple_of(i * step_rows, step_rows), step_rows)
            total = jnp.zeros((step_rows, features), jnp.float32)
            for t in range(n_tp):
                wide = toks[t, at, :].astype(jnp.float32)
                total = total + wide * wide
            mean = jnp.sum(total, axis=1, keepdims=True) / (n_tp * features)
            scale = lax.rsqrt(mean + 1e-06)
            for t in range(n_tp):
                wide = toks[t, at, :].astype(jnp.float32)
                value = (wide * scale * gains[t]).astype(jnp.bfloat16)
                for j in range(features // depth):
                    nrm[t * (features // depth) + j, at, :] = value[:, j * depth : (j + 1) * depth]
            return carry

        lax.fori_loop(0, rows // step_rows, some_rows, 0)

    def origin(direction, step):
        return lax.rem(me + (n_seq - step if direction == 0 else step), n_seq)

    def dot(shard, weight):
        return jnp.dot(nrm[shard], weight, preferred_element_type=jnp.float32)

    def kv_product(step):
        if step == 0:
            acc[...] += dot(me, wkv_ref[...])
            return
        total = dot(origin(0, step), wkvb[2 * step - 1])
        if step <= n_l:
            total = total + dot(origin(1, step), wkvb[2 * step])
        acc[...] += total

    def q_product(which, step):
        out, buffer = ((q0_ref, wqb0), (q1_ref, wqb1))[which]
        if step == 0:
            own = wq_ref[:, :, which * q_cols : (which + 1) * q_cols]
            out[...] += dot(me, own.reshape(depth, q_cols))
            return
        total = dot(origin(0, step), buffer[2 * step - 1].reshape(depth, q_cols))
        if step <= n_l:
            total = total + dot(origin(1, step), buffer[2 * step].reshape(depth, q_cols))
        out[...] += total

    def finish_kv():
        pair = acc[...] + bkv_ref[...]
        key, value = pair[:, :HEAD_DIM], pair[:, HEAD_DIM:]
        turned = key * cos_ref[...] + pltpu.roll(key, HEAD_DIM // 2, 1) * sin_ref[...]
        key = turned * live_ref[...]
        value = value * live_ref[...]
        knew_ref[...] = key.astype(jnp.bfloat16)
        vnew_ref[...] = value.astype(jnp.bfloat16)
        pages = rows // PAGE
        newp[pl.ds(0, pages), 0] = key.reshape(pages, PAGE, HEAD_DIM).astype(jnp.bfloat16)
        newp[pl.ds(0, pages), 1] = value.reshape(pages, PAGE, HEAD_DIM).astype(jnp.bfloat16)
        newp[pages] = jnp.zeros((2, PAGE, HEAD_DIM), jnp.bfloat16)

        cap = fsend.shape[1]

        def select(i, carry):
            for c in range(cap):
                fsend[i, c] = newp[source_ref[i * cap + c]]
            return carry

        lax.fori_loop(0, n_seq, select, 0)
        fresh_ref[me] = fsend[0]

    pending = []
    y_max = max(y_r, y_l)
    fresh_from = n_r + 1
    last = max(2 * n_r + 1 + y_max, n_r + PREFIX_LAG, fresh_from + n_r)
    for it in range(1, last + 1):
        for d in (0, 1):
            if it <= n_r:
                kv[d].arrive(it)
                kv[d].start(it + 1)
        for w in (0, 1):
            step = it - w * n_r
            if w == 1 and step == 0:
                for d in (0, 1):
                    q_ring[1][d].start(1)
            if 1 <= step <= n_r:
                for d in (0, 1):
                    q_ring[w][d].arrive(step)
                    q_ring[w][d].start(step + 1)
                for d in (0, 1):
                    y_start(w, step, d, 1)
        step = it - PREFIX_LAG
        if step == 0:
            for d in (0, 1):
                prefix[d].start(1)
        if 1 <= step <= n_r:
            for d in (0, 1):
                prefix[d].arrive(step)
                prefix[d].start(step + 1)
            got_ref[2 * step - 1] = pg_r[starts_r[step - 1]]
            if step <= n_l:
                got_ref[2 * step] = pg_l[starts_l[step - 1]]
        step = it - fresh_from
        if 1 <= step <= n_r:
            for d in (0, 1):
                fresh[d].arrive(step)
                fresh[d].start(step + 1)
            fresh_ref[origin(0, step)] = fg_r[starts_r[step - 1]]
            if step <= n_l:
                fresh_ref[origin(1, step)] = fg_l[starts_l[step - 1]]
        for hop in range(1, y_max + 1):
            for w in (0, 1):
                step = it - w * n_r - hop
                if 1 <= step <= n_r:
                    for d in (0, 1):
                        y_arrive(w, step, d, hop)
                        y_start(w, step, d, hop + 1)
        if it == 1:
            pending += [("kv", 0), (0, 0), (1, 0)]
        if it <= n_r:
            pending.append(("kv", it))
        for w in (0, 1):
            step = it - w * n_r - y_max
            if 1 <= step <= n_r:
                pending.append((w, step))
        if it == 3:
            tokens_near()
        if it == NORM_AT - 1:
            tokens_far()
        if it == NORM_AT:
            normalise()
        if it > NORM_AT:
            if it == n_r:
                pending.sort(key=lambda item: item[0] != "kv")
            take = len([1 for item in pending if item[0] == "kv"]) if it == n_r else 0
            take = len(pending) if it == last else max(take, CATCH_UP)
            for kind, step in pending[:take]:
                if kind == "kv":
                    kv_product(step)
                else:
                    q_product(kind, step)
            pending = pending[take:]
        if it == n_r:
            finish_kv()
        if it == fresh_from:
            for d in (0, 1):
                fresh[d].start(1)

    for pair in [kv, *q_ring, prefix, fresh]:
        for one in pair:
            one.drain()
    for copy in [*y_open.values(), *tok_open, *gain_open]:
        copy.wait_send()


def attend_kernel(
    q0_ref, q1_ref, bq_ref, cos_ref, sin_ref, knew_ref, vnew_ref, got_ref, at_ref, plen_ref, slen_ref,
    out_ref, kall, vall,
):
    rows = q0_ref.shape[0]
    requests = rows // BLOCK
    slots = at_ref.shape[0] // requests
    old = slots * PAGE
    per = q0_ref.shape[1] // HEAD_DIM
    for b in range(requests):
        def page(j, carry):
            index = at_ref[b * slots + j]
            to = pl.ds(pl.multiple_of(j * PAGE, PAGE), PAGE)
            kall[b, to, :] = got_ref[index, 0].astype(jnp.float32)
            vall[b, to, :] = got_ref[index, 1].astype(jnp.float32)
            return carry

        lax.fori_loop(0, slots, page, 0)
        mine = slice(b * BLOCK, (b + 1) * BLOCK)
        kall[b, old:, :] = knew_ref[mine, :].astype(jnp.float32)
        vall[b, old:, :] = vnew_ref[mine, :].astype(jnp.float32)
        keys = kall[b].astype(jnp.bfloat16)
        values = vall[b].astype(jnp.bfloat16)
        key_pos = lax.broadcasted_iota(jnp.int32, (BLOCK, old + BLOCK), 1)
        query_pos = lax.broadcasted_iota(jnp.int32, (BLOCK, old + BLOCK), 0)
        shifted = key_pos - old
        allowed = ((shifted < 0) & (key_pos < plen_ref[b])) | (
            (shifted >= 0) & (shifted <= query_pos) & (shifted < slen_ref[b])
        )
        live = lax.broadcasted_iota(jnp.int32, (BLOCK, HEAD_DIM), 0) < slen_ref[b]
        cos, sin = cos_ref[mine, :], sin_ref[mine, :]
        for h in range(2 * per):
            lin = (q0_ref, q1_ref)[h // per][mine, (h % per) * HEAD_DIM : (h % per + 1) * HEAD_DIM]
            lin = lin + bq_ref[:, h * HEAD_DIM : (h + 1) * HEAD_DIM]
            query = (lin * cos + pltpu.roll(lin, HEAD_DIM // 2, 1) * sin).astype(jnp.bfloat16)
            scores = lax.dot_general(
                query, keys, (((1,), (1,)), ((), ())), preferred_element_type=jnp.float32
            ) * (1.0 / math.sqrt(HEAD_DIM))
            masked = jnp.where(allowed, scores, -1e30)
            peak = jnp.max(masked, axis=1, keepdims=True)
            weights = jnp.where(allowed, jnp.exp(masked - peak), 0.0)
            probs = (weights / jnp.sum(weights, axis=1, keepdims=True)).astype(jnp.bfloat16)
            mixed = jnp.dot(probs, values, preferred_element_type=jnp.float32)
            out_ref[mine, h * HEAD_DIM : (h + 1) * HEAD_DIM] = jnp.where(live, mixed, 0.0).astype(
                jnp.bfloat16
            )


def body(
    n_parts,
    tokens, norm_gain, w_query, w_kv, b_query, b_kv, kv_pool, prefix_pages, prefix_len, suffix_len,
    fresh_owner,
):
    n_seq, n_tp = lax.axis_size("seq"), lax.axis_size("tp")
    me = lax.axis_index("seq")
    rows, features = tokens.shape
    requests = rows // BLOCK
    depth, query_width = w_query.shape
    kv_width = w_kv.shape[2]
    pool_pages = kv_pool.shape[0]
    slots = prefix_pages.shape[1]
    entries = requests * slots
    suffix_pages = BLOCK // PAGE
    fresh_entries = requests * suffix_pages
    prefix_cap = max(3, entries // n_seq + 1)
    fresh_cap = max(2, (fresh_entries + n_seq - 1) // n_seq + 1)
    n_r, n_l = n_seq // 2, (n_seq - 1) // 2
    first_row = me * requests
    prefix_mine = lax.dynamic_slice_in_dim(prefix_len, first_row, requests)
    suffix_mine = lax.dynamic_slice_in_dim(suffix_len, first_row, requests)
    owners_mine = lax.dynamic_slice_in_dim(fresh_owner[:, 0], first_row * suffix_pages, fresh_entries)
    steps = jnp.asarray(
        [0] + list(range(1, n_r + 1)) + [n_seq - k for k in range(1, n_l + 1)], jnp.int32
    )
    around = lax.rem(me + steps, n_seq)

    all_ids = prefix_pages.reshape(n_seq, entries)
    all_owner = all_ids // pool_pages
    entry = jnp.arange(entries, dtype=jnp.int32)
    earlier = entry[None, :] < entry[:, None]
    mine_here = all_owner == me
    before = jnp.sum(
        (mine_here[:, None, :] & earlier[None]).astype(jnp.int32), axis=-1
    )
    cap_ids = jnp.arange(prefix_cap, dtype=jnp.int32)
    chosen = mine_here[:, None, :] & (before[:, None, :] == cap_ids[None, :, None])
    local_page = jnp.sum(jnp.where(chosen, (all_ids % pool_pages)[:, None, :], 0), axis=-1)
    prefix_send = kv_pool[local_page[around]]

    my_ids = lax.dynamic_index_in_dim(all_ids, me, 0, keepdims=False)
    my_owner = my_ids // pool_pages
    my_rank = jnp.sum(((my_owner[None, :] == my_owner[:, None]) & earlier).astype(jnp.int32), axis=1)
    distance = lax.rem(me - my_owner + n_seq, n_seq)
    place = jnp.where(
        distance == 0, 0, jnp.where(distance <= n_r, 2 * distance - 1, 2 * (n_seq - distance))
    )
    arrived_at = place * prefix_cap + my_rank

    fresh_ids = jnp.arange(fresh_entries, dtype=jnp.int32)
    fresh_rank = jnp.sum(
        (
            (owners_mine[None, :] == owners_mine[:, None])
            & (fresh_ids[None, :] < fresh_ids[:, None])
        ).astype(jnp.int32),
        axis=1,
    )
    placed = (owners_mine[None, None, :] == around[:, None, None]) & (
        fresh_rank[None, None, :] == jnp.arange(fresh_cap, dtype=jnp.int32)[None, :, None]
    )
    source = jnp.sum(jnp.where(placed, fresh_ids[None, None, :] - fresh_entries, 0), axis=-1)
    source = (source + fresh_entries).reshape(-1)

    half_dim = HEAD_DIM // 2
    slot_ids = jnp.arange(BLOCK, dtype=jnp.int32)
    positions = (prefix_mine[:, None] + slot_ids[None, :]).reshape(rows, 1)
    inverse = jnp.exp(
        jnp.arange(half_dim, dtype=jnp.float32) * (-2.0 * math.log(1000000.0) / HEAD_DIM)
    )
    angles = positions.astype(jnp.float32) * inverse
    cosine, sine = jnp.cos(angles), jnp.sin(angles)
    cos_all = jnp.concatenate([cosine, cosine], axis=1)
    sin_all = jnp.concatenate([-sine, sine], axis=1)
    live = (slot_ids[None, :] < suffix_mine[:, None]).reshape(rows, 1)
    live_all = jnp.broadcast_to(live.astype(jnp.float32), (rows, HEAD_DIM))

    q_cols = query_width // 2
    piece = depth // n_parts
    y_lanes = max(1, n_parts - 1)
    tri_r, tri_l = offsets(n_r)[1], offsets(n_l)[1]
    page = (2, PAGE, HEAD_DIM)
    bf16, f32 = jnp.bfloat16, jnp.float32
    vmem = pl.BlockSpec(memory_space=pltpu.VMEM)
    smem = pl.BlockSpec(memory_space=pltpu.SMEM)
    dma = pltpu.SemaphoreType.DMA
    q0, q1, knew, vnew, got, fresh = pl.pallas_call(
        functools.partial(gather_kernel, n_parts, n_seq, n_tp),
        name="gather",
        out_shape=(
            jax.ShapeDtypeStruct((rows, q_cols), f32),
            jax.ShapeDtypeStruct((rows, q_cols), f32),
            jax.ShapeDtypeStruct((rows, HEAD_DIM), bf16),
            jax.ShapeDtypeStruct((rows, HEAD_DIM), bf16),
            jax.ShapeDtypeStruct((n_seq, prefix_cap, *page), bf16),
            jax.ShapeDtypeStruct((n_seq, fresh_cap, *page), bf16),
        ),
        in_specs=[vmem] * 9 + [smem],
        out_specs=(vmem,) * 6,
        scratch_shapes=[
            pltpu.VMEM((n_tp, rows, features), bf16),
            pltpu.VMEM((n_tp, 1, features), f32),
            pltpu.VMEM((n_seq, rows, depth), bf16),
            pltpu.VMEM((n_seq, depth, 2 * kv_width), bf16),
            pltpu.VMEM((n_seq, n_parts, piece, q_cols), bf16),
            pltpu.VMEM((n_seq, n_parts, piece, q_cols), bf16),
            pltpu.VMEM((rows, 2 * kv_width), f32),
            pltpu.VMEM((tri_r, prefix_cap, *page), bf16),
            pltpu.VMEM((tri_l, prefix_cap, *page), bf16),
            pltpu.VMEM((n_seq, fresh_cap, *page), bf16),
            pltpu.VMEM((tri_r, fresh_cap, *page), bf16),
            pltpu.VMEM((tri_l, fresh_cap, *page), bf16),
            pltpu.VMEM((fresh_entries + 1, *page), bf16),
            dma((5, 2, 2)),
            dma((5, 2, n_r)),
            dma((2, y_lanes, 2)),
            dma((2, y_lanes, n_r)),
            dma((9,)),
            dma((9,)),
            dma((n_tp - 1,)),
            dma((n_tp - 1,)),
        ],
        compiler_params=pltpu.CompilerParams(
            collective_id=0, has_side_effects=True, vmem_limit_bytes=60 * 1024 * 1024
        ),
    )(
        tokens,
        norm_gain.astype(f32).reshape(1, features),
        w_kv.reshape(depth, 2 * kv_width),
        w_query.reshape(n_parts, piece, query_width),
        b_kv.reshape(1, 2 * kv_width),
        cos_all,
        sin_all,
        live_all,
        prefix_send,
        source,
    )
    attn_out = pl.pallas_call(
        attend_kernel,
        name="attend",
        out_shape=jax.ShapeDtypeStruct((rows, query_width), bf16),
        in_specs=[vmem] * 8 + [smem] * 3,
        out_specs=vmem,
        scratch_shapes=[
            pltpu.VMEM((requests, slots * PAGE + BLOCK, HEAD_DIM), f32),
            pltpu.VMEM((requests, slots * PAGE + BLOCK, HEAD_DIM), f32),
        ],
    )(
        q0,
        q1,
        b_query.reshape(1, query_width),
        cos_all,
        sin_all,
        knew,
        vnew,
        got.reshape(n_seq * prefix_cap, *page),
        arrived_at,
        prefix_mine,
        suffix_mine,
    )
    return attn_out, fresh.reshape(n_seq * fresh_cap, *page)


def solution(mesh):
    placed = (
        P(("parts", "seq"), "tp"),
        P("tp"),
        P("seq", "tp"),
        P("seq", None, "tp"),
        P("tp"),
        P(None, "tp"),
        P(("parts", "seq"), None, None, "tp"),
        P("parts", None),
        P("parts"),
        P("parts"),
        P("parts", None),
    )
    return jax.shard_map(
        functools.partial(body, mesh.shape["parts"]),
        mesh=mesh,
        in_specs=placed,
        out_specs=(P(("parts", "seq"), "tp"), P(("parts", "seq"), None, None, "tp")),
        check_vma=False,
    )
```

time: 324 us -> 241 us (0.74)
  Pallas kernels: 0 us -> 226 us
  waiting for transfers between devices: 210 us -> 0 us
  starting transfers between devices: 61.9 us -> 0 us
  between operations: 14.4 us -> 0.77 us
  matrix products: 12.8 us -> 0 us
  other arithmetic: 12.7 us -> 4.16 us
    pallas_call x0 -> x2, Pallas kernels: none -> 226 us  [the longest x1 221 us: body(): pl.pallas_call(functools.partial(gather_kernel, n_parts, n_seq, n_tp), na...]
    all_gather x2 -> x0, waiting for transfers between devices: 129 us -> none  [the longest x1 129 us: in_one_piece(): lax.all_gather(both, axis, axis=dim, tiled=True)]
    all_to_all x2 -> x0, waiting for transfers between devices: 81.1 us -> none  [the longest x1 50 us: body(): lax.all_to_all(prefix_send, 'seq', split_axis=0, concat_axis=0, tiled=True)]
    all_to_all x2 -> x0, starting transfers between devices: 61.8 us -> none  [the longest x1 45.8 us: body(): lax.all_to_all(prefix_send, 'seq', split_axis=0, concat_axis=0, tiled=True)]
    dot_general x4 -> x0, matrix products: 12.8 us -> none  [the longest x2 11.8 us: body(): jnp.dot(normed, weight_piece.reshape(weight_piece.shape[0], -1), preferre...]
    reduce_sum x6 -> x5, other arithmetic: 4.83 us -> 1.24 us  [the longest x1 0.62 us: body(): jnp.sum((mine_here[:, None, :] & earlier[None]).astype(jnp.int32), axis=-1)]
  transfers between devices with their start and end apart: 4 -> 0, of which waited for: 3 -> 0; matrix products, arithmetic and copies ran while one was open for 8% -> 0% of each run, Pallas kernels for 0% -> 0%
where the time goes in v1:
time: 241 us; the launch traced here: 240 us
  Pallas kernels  226 us (94%)
  local copies, waits for them, and re-layouts  9.18 us (4%)
  other arithmetic  4.16 us (2%)
    pallas_call x1, Pallas kernels, body(): pl.pallas_call(functools.partial(gather_kernel, n_parts, n_seq, n_tp), na...  221 us
    pallas_call x1, Pallas kernels, body(): pl.pallas_call(attend_kernel, name='attend', out_shape=jax.ShapeDtypeStru...  5.78 us

profile of v1, /device:TPU:40, one launch (start us, length us, event | category | flops | bytes accessed | tf_op | source)
XLA Modules:
  0.0 240.5 jit_solution(1970072703667573031)
XLA Ops:
  0.7 0.8 dynamic-slice_bitcast_fusion
  1.4 0.7 copy-done.8
  2.1 0.1 dynamic_slice.13.plen_ref
  2.2 0.6 copy-done.9
  2.8 0.1 dynamic_slice.14.slen_ref
  2.8 0.2 convert_reduce_fusion.2
  3.0 0.3 copy-done.6
  3.5 0.6 copy-done.7
  4.2 0.1 select_reduce_fusion.1
  4.3 0.7 copy-done.4
  5.0 0.6 reshape.255
  5.6 0.1 copy.23
  5.7 0.7 add.114.source_ref
  6.4 0.1 copy.19
  6.5 0.1 reshape.251
  6.6 0.2 convert_reduce_fusion.1
  6.8 0.6 fusion.9.at_ref
  7.4 0.6 convert_reduce_fusion
  8.0 0.1 select_reduce_fusion
  8.2 0.1 copy.20
  8.3 0.6 gather_fusion
  8.9 0.1 copy.21
  9.0 0.1 copy.22
  9.0 0.1 reshape.268
  9.2 0.8 broadcast_in_dim.26.live_ref
  9.9 0.7 copy.26
  10.6 1.4 gather_fusion.1
  12.0 0.5 fusion.1
  12.5 0.8 pad_maximum_fusion
  13.4 220.6 %gather.16 = (f32[256,256]{1,0:T(8,128)}, f32[256,256]{1,0:T(8,128)}, bf16[256,128]{1,0:T(8,128)(2,1)}, bf16[256,128]{1,0:T(8,128)(2,1)}, bf16[32,3,2,8,128]{4,3...) custom-call(bf16[256,1024]{1,0:T(8,128)(2,1)} %tok_ref.1, f32[1,1024]{1,0:T(1,128)} %bitcast.39, ...), custom_call_target="tpu_custom_call" | custom-call | tf_op jit(solution)/shard_map/gather/pallas_call | solution.py:536
  234.0 5.8 %attend.1 = bf16[256,512]{1,0:T(8,128)(2,1)} custom-call(f32[256,256]{1,0:T(8,128)} %get-tuple-element.8.q0_ref, f32[256,256]{1,0:T(8,128)} %get-tuple-element.9.q1_ref, f32[1,512]{1,0:T(1,128)} %bitcast.40, f32[256,128]{1,0:T(8,128)} %get-tuple-element.19.cos_ref, f32[256,128]{1,0:T(8,128)} %get-tuple-element.20.sin_ref, ...), custom_call_target="tpu_custom_call" | custom-call | tf_op jit(solution)/shard_map/attend/pallas_call | solution.py:587
  239.8 0.7 copy.28
  (31 shorter events, 0.4 us)
Async XLA Ops:
  0.6 10.0 %copy-start = (bf16[128,2,8,128]{3,2,1,0:T(8,128)(2,1)S(1)}, bf16[128,2,8,128]{3,2,1,0:T(8,128)(2,1)}, u32[]{:S(2)}) copy-start(bf16[128,2,8,128]{3,2,1,0:T(8,128)(2,1)} %param.18) | copy-start | bytes 1572868
  1.4 0.7 copy-start.8
  2.1 0.7 copy-start.9
  2.7 0.7 copy-start.5
  2.8 0.5 copy-start.6
  3.4 0.7 copy-start.7
  4.3 0.7 copy-start.4
  5.6 0.8 copy-start.3
  8.9 1.1 copy-start.2
  234.0 5.8 %copy-start.1 = (bf16[32,2,2,8,128]{4,3,2,1,0:T(8,128)(2,1)S(1)}, bf16[32,2,2,8,128]{4,3,2,1,0:T(8,128)(2,1)}, u32[]{:S(2)}) copy-start(bf16[32,2,2,8,128]{4,3,2,1,0:T(8,128)(2,1)} %get-tuple-element.13) | copy-start | bytes 786436

commit v2 on v1

v2 whole, which is shorter than its diff:
```python
import functools
import math

import jax
import jax.numpy as jnp
from jax import lax
from jax.experimental import pallas as pl
from jax.experimental.pallas import tpu as pltpu
from jax.sharding import PartitionSpec as P

HEAD_DIM = 128
BLOCK = 128
PAGE = 8
MESH = pl.DeviceIdType.MESH

PREFIX_LAG = 6
Z_LAG = (0, 1, 3)
Y_WAIT = (0, 0, 8)
GROUPS_AT_ONCE = 2


def offsets(count):
    starts, at = [], 0
    for step in range(1, count + 1):
        starts.append(at)
        at += count - step + 1
    return starts, at


class Ring:
    def __init__(self, make, steps):
        self.make, self.steps, self.started = make, steps, {}

    def start(self, step):
        if step > self.steps:
            return
        if step > 2:
            self.started.pop(step - 2).wait_send()
        copy = self.make(step)
        copy.start()
        self.started[step] = copy

    def arrive(self, step):
        if step <= self.steps:
            self.make(step).wait_recv()

    def drain(self):
        for copy in self.started.values():
            copy.wait_send()
        self.started = {}


def gather_kernel(
    n_parts, n_seq, n_tp,
    tok_ref, gain_ref, wkv_ref, wq_ref, bkv_ref, cos_ref, sin_ref, pool_ref,
    pages_ref, plen_ref, slen_ref, owner_ref,
    q0_ref, q1_ref, knew_ref, vnew_ref, got_ref, fresh_ref,
    toks, gains, nrm, wkvb, wqb0, wqb1, acc, psend, pg_r, pg_l, fsend, fgot, newp, source,
    ring_send, ring_recv, y_send, y_recv, tok_send, tok_recv, gain_send, gain_recv,
    fresh_send, fresh_recv,
):
    part, me, tp = lax.axis_index("parts"), lax.axis_index("seq"), lax.axis_index("tp")
    right, left = lax.rem(me + 1, n_seq), lax.rem(me + n_seq - 1, n_seq)
    up, down = lax.rem(part + 1, n_parts), lax.rem(part + n_parts - 1, n_parts)
    n_r, n_l = n_seq // 2, (n_seq - 1) // 2
    y_r, y_l = n_parts // 2, (n_parts - 1) // 2
    y_max = max(y_r, y_l)
    partner = tp + 1 - 2 * lax.rem(tp, 2)
    x_right, x_left = lax.rem(tp + 2, n_tp), lax.rem(tp + n_tp - 2, n_tp)
    x_far = lax.rem(tp + n_tp // 2, n_tp)
    rows, features = tok_ref.shape
    half = rows // 2
    depth = wkv_ref.shape[0] * wkv_ref.shape[1]
    q_cols = q0_ref.shape[1]
    pool_pages = pool_ref.shape[0]
    requests = rows // BLOCK
    fresh_entries = rows // PAGE
    prefix_cap, fresh_cap = psend.shape[1], fsend.shape[1]

    barrier = pltpu.get_barrier_semaphore()
    greeted = [{"seq": right}, {"seq": left}]
    greeted += [{"tp": lax.rem(tp + r, n_tp)} for r in range(1, n_tp)]
    if n_parts > 1:
        greeted.append({"parts": up})
    if n_parts > 2:
        greeted.append({"parts": down})
    for device in greeted:
        pl.semaphore_signal(barrier, inc=1, device_id=device, device_id_type=MESH)
    pl.semaphore_wait(barrier, len(greeted))

    def remote(src, dst, send, recv, device):
        return pltpu.make_async_remote_copy(
            src_ref=src, dst_ref=dst, send_sem=send, recv_sem=recv,
            device_id=device, device_id_type=MESH,
        )

    def origin(direction, step):
        return lax.rem(me + (n_seq - step if direction == 0 else step), n_seq)

    def around(index):
        by = jnp.where(index <= n_r, index, n_seq + n_r - index)
        return lax.rem(me + by, n_seq)

    def slot(direction, step):
        return 2 * step - 1 if direction == 0 else 2 * step

    def ring(stream, direction, make_refs):
        target = {"seq": right if direction == 0 else left}

        def make(step):
            src, dst = make_refs(step)
            return remote(
                src, dst, ring_send.at[stream, direction, step % 2],
                ring_recv.at[stream, direction, step - 1], target,
            )

        return Ring(make, n_r if direction == 0 else n_l)

    buffers = (wkvb, wqb0, wqb1)
    owns = (
        lambda: wkv_ref.at[part],
        lambda: wq_ref.at[part, :, pl.ds(0, q_cols)],
        lambda: wq_ref.at[part, :, pl.ds(q_cols, q_cols)],
    )

    def weight_refs(which, direction):
        def refs(step):
            if step == 1:
                src = owns[which]()
            else:
                src = buffers[which].at[slot(direction, step - 1), part]
            return src, buffers[which].at[slot(direction, step), part]

        return refs

    starts = (offsets(n_r)[0], offsets(n_l)[0])

    def prefix_refs(direction):
        count, buffer = ((n_r, pg_r), (n_l, pg_l))[direction]

        def refs(step):
            size = count - step + 1
            if step == 1:
                src = psend.at[pl.ds(1 if direction == 0 else 1 + n_r, count)]
            else:
                src = buffer.at[pl.ds(starts[direction][step - 2] + 1, size)]
            return src, buffer.at[pl.ds(starts[direction][step - 1], size)]

        return refs

    weights = [[ring(w, d, weight_refs(w, d)) for d in (0, 1)] for w in range(3)]
    prefix = [ring(3, d, prefix_refs(d)) for d in (0, 1)]

    y_open = {}

    def y_make(which, step, direction, hop, behind):
        by = hop - 1 + behind
        piece = lax.rem(part + (n_parts - by if direction == 0 else by), n_parts)
        pair = pl.ds(2 * step - 1, 2 if step <= n_l else 1)
        ref = buffers[which].at[pair, piece]
        lane = hop - 1 if direction == 0 else y_r + hop - 1
        return remote(
            ref, ref, y_send.at[which, lane, step % 2], y_recv.at[which, lane, step - 1],
            {"parts": up if direction == 0 else down},
        )

    def y_start(which, step, direction, hop):
        if hop > (y_r if direction == 0 else y_l):
            return
        key = (which, direction, hop)
        if (key, step - 2) in y_open:
            y_open.pop((key, step - 2)).wait_send()
        copy = y_make(which, step, direction, hop, 0)
        copy.start()
        y_open[(key, step)] = copy

    def y_arrive(which, step, direction, hop):
        if hop <= (y_r if direction == 0 else y_l):
            y_make(which, step, direction, hop, 1).wait_recv()

    lo, hi = pl.ds(0, half), pl.ds(half, half)

    def tok_copy(index, src, block, part_rows, device):
        dst = toks.at[block] if part_rows is None else toks.at[block, part_rows]
        if src is None:
            src = dst
        return remote(src, dst, tok_send.at[index], tok_recv.at[index], {"tp": device})

    opened = []

    def tok_start(*args):
        copy = tok_copy(*args)
        copy.start()
        opened.append(copy)

    for d in (0, 1):
        weights[0][d].start(1)
    tok_start(1, tok_ref, tp, None, x_right)
    tok_start(2, tok_ref, tp, None, x_left)
    tok_start(0, tok_ref, tp, None, partner)
    for r in range(1, n_tp):
        copy = remote(
            gain_ref, gains.at[tp], gain_send.at[r - 1], gain_recv.at[r - 1],
            {"tp": lax.rem(tp + r, n_tp)},
        )
        copy.start()
        opened.append(copy)
    toks[tp] = tok_ref[...]
    gains[tp] = gain_ref[...]
    acc[...] = jnp.zeros_like(acc)
    q0_ref[...] = jnp.zeros_like(q0_ref)
    q1_ref[...] = jnp.zeros_like(q1_ref)

    def tokens_near():
        tok_copy(1, None, x_left, None, x_right).wait_recv()
        tok_start(5, None, x_left, lo, x_right)
        tok_start(3, None, x_left, None, partner)
        tok_copy(2, None, x_right, None, x_left).wait_recv()
        tok_start(6, None, x_right, hi, x_left)
        tok_start(4, None, x_right, None, partner)

    def tokens_far():
        tok_copy(5, None, x_far, lo, x_right).wait_recv()
        tok_start(7, None, x_far, lo, partner)
        tok_copy(6, None, x_far, hi, x_left).wait_recv()
        tok_start(8, None, x_far, hi, partner)

    def shifted(base, by):
        return lax.rem(base + by, n_tp)

    def tokens_here():
        p_left, p_right = shifted(partner, n_tp - 2), shifted(partner, 2)
        p_far = shifted(partner, n_tp // 2)
        for index, block, part_rows in (
            (0, partner, None), (3, p_left, None), (4, p_right, None),
            (7, p_far, lo), (8, p_far, hi),
        ):
            tok_copy(index, None, block, part_rows, partner).wait_recv()
        for r in range(1, n_tp):
            remote(
                gain_ref, gains.at[lax.rem(tp + n_tp - r, n_tp)],
                gain_send.at[r - 1], gain_recv.at[r - 1], {"tp": lax.rem(tp + r, n_tp)},
            ).wait_recv()

    def normalise(first, count):
        step_rows = 16

        def some_rows(i, carry):
            at = pl.ds(pl.multiple_of(i * step_rows, step_rows), step_rows)
            total = jnp.zeros((step_rows, features), jnp.float32)
            for t in range(n_tp):
                wide = toks[t, at, :].astype(jnp.float32)
                total = total + wide * wide
            mean = jnp.sum(total, axis=1, keepdims=True) / (n_tp * features)
            scale = lax.rsqrt(mean + 1e-06)
            for t in range(n_tp):
                wide = toks[t, at, :].astype(jnp.float32)
                value = (wide * scale * gains[t]).astype(jnp.bfloat16)
                for j in range(features // depth):
                    nrm[t * (features // depth) + j, at, :] = value[:, j * depth : (j + 1) * depth]
            return carry

        lax.fori_loop(first // step_rows, (first + count) // step_rows, some_rows, 0)

    def dot(shard, weight):
        return jnp.dot(
            nrm[shard], weight.reshape(depth, -1), preferred_element_type=jnp.float32
        )

    sums = (acc, q0_ref, q1_ref)
    done = [0, 0, 0]

    def product(which, step):
        done[which] += 1
        if step == 0:
            own = wkv_ref[...] if which == 0 else wq_ref[:, :, (which - 1) * q_cols : which * q_cols]
            sums[which][...] += dot(me, own)
            return
        total = dot(origin(0, step), buffers[which][2 * step - 1])
        if step <= n_l:
            total = total + dot(origin(1, step), buffers[which][2 * step])
        sums[which][...] += total

    def pick_pages(first):
        def one(index, carry):
            group = around(index)

            def entry(j, state):
                count, picks = state
                for r in range(requests):
                    local = pages_ref[j, group * requests + r] - me * pool_pages
                    hit = jnp.where((local >= 0) & (local < pool_pages), 1, 0)
                    picks = tuple(
                        jnp.where((hit == 1) & (count == c), local, p) for c, p in enumerate(picks)
                    )
                    count = count + hit
                return count, picks

            zero = jnp.int32(0)
            _, picks = lax.fori_loop(
                0, pages_ref.shape[0], entry, (zero, (zero,) * prefix_cap), unroll=4
            )
            for c in range(prefix_cap):
                psend[index, c] = pool_ref[picks[c]]
            return carry

        lax.fori_loop(first, first + GROUPS_AT_ONCE, one, 0)

    def pick_source(first):
        def one(index, carry):
            group = around(index)

            def entry(e, state):
                count, picks = state
                hit = jnp.where(owner_ref[me * fresh_entries + e] == group, 1, 0)
                picks = tuple(
                    jnp.where((hit == 1) & (count == c), e, p) for c, p in enumerate(picks)
                )
                return count + hit, picks

            none = jnp.int32(fresh_entries)
            _, picks = lax.fori_loop(
                0, fresh_entries, entry, (jnp.int32(0), (none,) * fresh_cap), unroll=4
            )
            for c in range(fresh_cap):
                source[index * fresh_cap + c] = picks[c]
            return carry

        lax.fori_loop(first, first + GROUPS_AT_ONCE, one, 0)

    def finish_kv():
        for b in range(requests):
            mine = slice(b * BLOCK, (b + 1) * BLOCK)
            pair = acc[mine, :] + bkv_ref[...]
            key, value = pair[:, :HEAD_DIM], pair[:, HEAD_DIM:]
            at = pl.ds(plen_ref[me * requests + b], BLOCK)
            turned = key * cos_ref[at, :] + pltpu.roll(key, HEAD_DIM // 2, 1) * sin_ref[at, :]
            index = lax.broadcasted_iota(jnp.int32, (BLOCK, HEAD_DIM), 0)
            live = index < slen_ref[me * requests + b]
            key = jnp.where(live, turned, 0.0)
            value = jnp.where(live, value, 0.0)
            knew_ref[mine, :] = key.astype(jnp.bfloat16)
            vnew_ref[mine, :] = value.astype(jnp.bfloat16)
            count = BLOCK // PAGE
            pages = pl.ds(b * count, count)
            newp[pages, 0] = key.reshape(count, PAGE, HEAD_DIM).astype(jnp.bfloat16)
            newp[pages, 1] = value.reshape(count, PAGE, HEAD_DIM).astype(jnp.bfloat16)
        newp[fresh_entries] = jnp.zeros((2, PAGE, HEAD_DIM), jnp.bfloat16)

        def select(i, carry):
            for c in range(fresh_cap):
                fsend[i, c] = newp[source[i * fresh_cap + c]]
            return carry

        lax.fori_loop(0, n_seq, select, 0)
        fgot[me] = fsend[0]

    def fresh_copy(direction, step, behind):
        index = step if direction == 0 else n_r + step
        group = origin(1 - direction, step)
        there = me if not behind else origin(direction, step)
        return remote(
            fsend.at[index], fgot.at[there], fresh_send.at[index - 1], fresh_recv.at[index - 1],
            {"seq": group},
        )

    far_first = [
        (d, step) for step in range(n_r, 0, -1) for d in (0, 1) if step <= (n_r if d == 0 else n_l)
    ]

    work = []

    def fill(count):
        for _ in range(min(count, len(work))):
            work.pop(0)()

    work += [functools.partial(pick_pages, i) for i in range(0, n_seq, GROUPS_AT_ONCE)]
    sources = [functools.partial(pick_source, i) for i in range(0, n_seq, GROUPS_AT_ONCE)]
    products = []

    def compute(count):
        for _ in range(min(count, len(products))):
            product(*products.pop(0))

    wait = y_max + 1 if y_max else 0
    kv_end = n_r + Z_LAG[0] + Y_WAIT[0] + wait
    last = max(max(n_r + z + y + wait for z, y in zip(Z_LAG, Y_WAIT)), n_r + PREFIX_LAG)
    ready = 7
    for it in range(1, last + 1):
        busy = compute if it > ready else fill
        for w in range(3):
            step = it - Z_LAG[w]
            if step == 0:
                for d in (0, 1):
                    weights[w][d].start(1)
            if 1 <= step <= n_r:
                for d in (0, 1):
                    weights[w][d].arrive(step)
                    weights[w][d].start(step + 1)
            step -= Y_WAIT[w]
            if 1 <= step <= n_r:
                for d in (0, 1):
                    y_start(w, step, d, 1)
            busy(1)
        step = it - PREFIX_LAG
        if step == 0:
            fill(len(work))
            got_ref[0] = psend[0]
            for d in (0, 1):
                prefix[d].start(1)
            work += sources
        if 1 <= step <= n_r:
            for d in (0, 1):
                prefix[d].arrive(step)
                prefix[d].start(step + 1)
            got_ref[2 * step - 1] = pg_r[starts[0][step - 1]]
            if step <= n_l:
                got_ref[2 * step] = pg_l[starts[1][step - 1]]
        busy(1)
        for w in range(3):
            for hop in range(1, y_max + 1):
                step = it - Z_LAG[w] - Y_WAIT[w] - hop - 1
                if 1 <= step <= n_r:
                    for d in (0, 1):
                        y_arrive(w, step, d, hop)
                        y_start(w, step, d, hop + 1)
            step = it - Z_LAG[w] - Y_WAIT[w] - wait
            if 0 <= step <= n_r:
                products.append((w, step))
        if it == 3:
            tokens_near()
        if it == ready - 2:
            tokens_far()
        if it == ready - 1:
            tokens_here()
            normalise(0, half)
        if it == ready:
            normalise(half, half)
        if it > ready:
            fill(1)
        if it == kv_end:
            fill(len(work))
            products.sort(key=lambda item: item[0])
            compute(len([item for item in products if item[0] == 0]))
            finish_kv()
            for d, step in far_first:
                copy = fresh_copy(d, step, False)
                copy.start()
                opened.append(copy)
    compute(len(products))
    assert done == [n_r + 1] * 3 and not work

    for d, step in far_first:
        fresh_copy(d, step, True).wait_recv()
    fresh_ref[...] = fgot[...]
    for pair in [*weights, prefix]:
        for one in pair:
            one.drain()
    for copy in [*y_open.values(), *opened]:
        copy.wait_send()


def attend_kernel(
    n_seq, pool_pages,
    q0_ref, q1_ref, bq_ref, cos_ref, sin_ref, knew_ref, vnew_ref, got_ref,
    pages_ref, plen_ref, slen_ref,
    out_ref, kall, vall, counts,
):
    me = lax.axis_index("seq")
    rows = q0_ref.shape[0]
    requests = rows // BLOCK
    slots = pages_ref.shape[0]
    old = slots * PAGE
    per = q0_ref.shape[1] // HEAD_DIM
    cap = got_ref.shape[0] // n_seq
    n_r = n_seq // 2

    def clear(i, carry):
        counts[i] = 0
        return carry

    lax.fori_loop(0, n_seq, clear, 0)

    def page(j, carry):
        to = pl.ds(pl.multiple_of(j * PAGE, PAGE), PAGE)
        for b in range(requests):
            owner = lax.div(pages_ref[j, me * requests + b], pool_pages)
            rank = counts[owner]
            counts[owner] = rank + 1
            away = me - owner
            away = jnp.where(away < 0, away + n_seq, away)
            place = jnp.where(away <= n_r, 2 * away - 1, 2 * (n_seq - away))
            place = jnp.where(away == 0, 0, place)
            index = place * cap + rank
            kall[b, to, :] = got_ref[index, 0].astype(jnp.float32)
            vall[b, to, :] = got_ref[index, 1].astype(jnp.float32)
        return carry

    lax.fori_loop(0, slots, page, 0, unroll=4)
    for b in range(requests):
        mine = slice(b * BLOCK, (b + 1) * BLOCK)
        kall[b, old:, :] = knew_ref[mine, :].astype(jnp.float32)
        vall[b, old:, :] = vnew_ref[mine, :].astype(jnp.float32)
        keys = kall[b].astype(jnp.bfloat16)
        values = vall[b].astype(jnp.bfloat16)
        here = me * requests + b
        key_pos = lax.broadcasted_iota(jnp.int32, (BLOCK, old + BLOCK), 1)
        query_pos = lax.broadcasted_iota(jnp.int32, (BLOCK, old + BLOCK), 0)
        shifted = key_pos - old
        allowed = ((shifted < 0) & (key_pos < plen_ref[here])) | (
            (shifted >= 0) & (shifted <= query_pos) & (shifted < slen_ref[here])
        )
        live = lax.broadcasted_iota(jnp.int32, (BLOCK, HEAD_DIM), 0) < slen_ref[here]
        at = pl.ds(plen_ref[here], BLOCK)
        cos, sin = cos_ref[at, :], sin_ref[at, :]
        for h in range(2 * per):
            lin = (q0_ref, q1_ref)[h // per][mine, (h % per) * HEAD_DIM : (h % per + 1) * HEAD_DIM]
            lin = lin + bq_ref[:, h * HEAD_DIM : (h + 1) * HEAD_DIM]
            query = (lin * cos + pltpu.roll(lin, HEAD_DIM // 2, 1) * sin).astype(jnp.bfloat16)
            scores = lax.dot_general(
                query, keys, (((1,), (1,)), ((), ())), preferred_element_type=jnp.float32
            ) * (1.0 / math.sqrt(HEAD_DIM))
            masked = jnp.where(allowed, scores, -1e30)
            peak = jnp.max(masked, axis=1, keepdims=True)
            weights = jnp.where(allowed, jnp.exp(masked - peak), 0.0)
            probs = (weights * (1.0 / jnp.sum(weights, axis=1, keepdims=True))).astype(jnp.bfloat16)
            mixed = jnp.dot(probs, values, preferred_element_type=jnp.float32)
            out_ref[mine, h * HEAD_DIM : (h + 1) * HEAD_DIM] = jnp.where(live, mixed, 0.0).astype(
                jnp.bfloat16
            )


def body(
    n_parts,
    tokens, norm_gain, w_query, w_kv, b_query, b_kv, kv_pool, prefix_pages, prefix_len, suffix_len,
    fresh_owner,
):
    n_seq, n_tp = lax.axis_size("seq"), lax.axis_size("tp")
    rows, features = tokens.shape
    requests = rows // BLOCK
    depth, query_width = w_query.shape
    kv_width = w_kv.shape[2]
    pool_pages = kv_pool.shape[0]
    slots = prefix_pages.shape[1]
    entries = requests * slots
    fresh_entries = rows // PAGE
    prefix_cap = max(3, entries // n_seq + 1)
    fresh_cap = max(2, (fresh_entries + n_seq - 1) // n_seq + 1)
    n_r, n_l = n_seq // 2, (n_seq - 1) // 2

    half_dim = HEAD_DIM // 2
    positions = jnp.arange(slots * PAGE + BLOCK, dtype=jnp.float32)[:, None]
    inverse = jnp.exp(
        jnp.arange(half_dim, dtype=jnp.float32) * (-2.0 * math.log(1000000.0) / HEAD_DIM)
    )
    angles = positions * inverse
    cosine, sine = jnp.cos(angles), jnp.sin(angles)
    cos_all = jnp.concatenate([cosine, cosine], axis=1)
    sin_all = jnp.concatenate([-sine, sine], axis=1)
    pages_by_slot = prefix_pages.T

    q_cols = query_width // 2
    piece = depth // n_parts
    y_lanes = max(1, n_parts - 1)
    tri_r, tri_l = offsets(n_r)[1], offsets(n_l)[1]
    page = (2, PAGE, HEAD_DIM)
    bf16, f32 = jnp.bfloat16, jnp.float32
    vmem = pl.BlockSpec(memory_space=pltpu.VMEM)
    smem = pl.BlockSpec(memory_space=pltpu.SMEM)
    dma = pltpu.SemaphoreType.DMA
    q0, q1, knew, vnew, got, fresh = pl.pallas_call(
        functools.partial(gather_kernel, n_parts, n_seq, n_tp),
        name="gather",
        out_shape=(
            jax.ShapeDtypeStruct((rows, q_cols), f32),
            jax.ShapeDtypeStruct((rows, q_cols), f32),
            jax.ShapeDtypeStruct((rows, HEAD_DIM), bf16),
            jax.ShapeDtypeStruct((rows, HEAD_DIM), bf16),
            jax.ShapeDtypeStruct((n_seq, prefix_cap, *page), bf16),
            jax.ShapeDtypeStruct((n_seq, fresh_cap, *page), bf16),
        ),
        in_specs=[vmem] * 8 + [smem] * 4,
        out_specs=(vmem,) * 6,
        scratch_shapes=[
            pltpu.VMEM((n_tp, rows, features), bf16),
            pltpu.VMEM((n_tp, 1, features), f32),
            pltpu.VMEM((n_seq, rows, depth), bf16),
            pltpu.VMEM((n_seq, n_parts, piece, 2 * kv_width), bf16),
            pltpu.VMEM((n_seq, n_parts, piece, q_cols), bf16),
            pltpu.VMEM((n_seq, n_parts, piece, q_cols), bf16),
            pltpu.VMEM((rows, 2 * kv_width), f32),
            pltpu.VMEM((n_seq, prefix_cap, *page), bf16),
            pltpu.VMEM((tri_r, prefix_cap, *page), bf16),
            pltpu.VMEM((tri_l, prefix_cap, *page), bf16),
            pltpu.VMEM((n_seq, fresh_cap, *page), bf16),
            pltpu.VMEM((n_seq, fresh_cap, *page), bf16),
            pltpu.VMEM((fresh_entries + 1, *page), bf16),
            pltpu.SMEM((n_seq * fresh_cap,), jnp.int32),
            dma((4, 2, 2)),
            dma((4, 2, n_r)),
            dma((3, y_lanes, 2)),
            dma((3, y_lanes, n_r)),
            dma((9,)),
            dma((9,)),
            dma((n_tp - 1,)),
            dma((n_tp - 1,)),
            dma((n_seq - 1,)),
            dma((n_seq - 1,)),
        ],
        compiler_params=pltpu.CompilerParams(
            collective_id=0, has_side_effects=True, vmem_limit_bytes=60 * 1024 * 1024
        ),
    )(
        tokens,
        norm_gain.astype(f32).reshape(1, features),
        w_kv.reshape(n_parts, piece, 2 * kv_width),
        w_query.reshape(n_parts, piece, query_width),
        b_kv.reshape(1, 2 * kv_width),
        cos_all,
        sin_all,
        kv_pool,
        pages_by_slot,
        prefix_len,
        suffix_len,
        fresh_owner.reshape(-1),
    )
    attn_out = pl.pallas_call(
        functools.partial(attend_kernel, n_seq, pool_pages),
        name="attend",
        out_shape=jax.ShapeDtypeStruct((rows, query_width), bf16),
        in_specs=[vmem] * 8 + [smem] * 3,
        out_specs=vmem,
        scratch_shapes=[
            pltpu.VMEM((requests, slots * PAGE + BLOCK, HEAD_DIM), f32),
            pltpu.VMEM((requests, slots * PAGE + BLOCK, HEAD_DIM), f32),
            pltpu.SMEM((n_seq,), jnp.int32),
        ],
    )(
        q0,
        q1,
        b_query.reshape(1, query_width),
        cos_all,
        sin_all,
        knew,
        vnew,
        got.reshape(n_seq * prefix_cap, *page),
        pages_by_slot,
        prefix_len,
        suffix_len,
    )
    return attn_out, fresh.reshape(n_seq * fresh_cap, *page)


def solution(mesh):
    placed = (
        P(("parts", "seq"), "tp"),
        P("tp"),
        P("seq", "tp"),
        P("seq", None, "tp"),
        P("tp"),
        P(None, "tp"),
        P(("parts", "seq"), None, None, "tp"),
        P("parts", None),
        P("parts"),
        P("parts"),
        P("parts", None),
    )
    return jax.shard_map(
        functools.partial(body, mesh.shape["parts"]),
        mesh=mesh,
        in_specs=placed,
        out_specs=(P(("parts", "seq"), "tp"), P(("parts", "seq"), None, None, "tp")),
        check_vma=False,
    )
```

time: 241 us -> 214 us (0.89)
  Pallas kernels: 226 us -> 207 us
  local copies, waits for them, and re-layouts: 9.18 us -> 3.01 us
    pallas_call x1, Pallas kernels: 221 us -> 201 us  [body(): pl.pallas_call(functools.partial(gather_kernel, n_parts, n_seq, n_tp), na...]
    unnamed x23 -> x5, local copies, waits for them, and re-layouts: 4.3 us -> 1.37 us
where the time goes in v2:
time: 214 us; the launch traced here: 213 us
  Pallas kernels  207 us (97%)
  local copies, waits for them, and re-layouts  3.01 us (1%)
  other arithmetic  2.28 us (1%)
    pallas_call x1, Pallas kernels, body(): pl.pallas_call(functools.partial(gather_kernel, n_parts, n_seq, n_tp), na...  201 us
    pallas_call x1, Pallas kernels, body(): pl.pallas_call(functools.partial(attend_kernel, n_seq, pool_pages), name=...  6.01 us

profile of v2, /device:TPU:40, one launch (start us, length us, event | category | flops | bytes accessed | tf_op | source)
XLA Modules:
  0.0 212.6 jit_solution(6263586094990493295)
XLA Ops:
  0.6 0.0 copy-start.1
  0.7 0.7 copy-done.1
  1.3 0.6 reshape.44
  1.9 1.6 reshape.37.wkv_ref
  3.6 0.7 fusion.2
  4.3 0.9 pad_maximum_fusion
  5.2 200.7 %gather.1 = (f32[256,256]{1,0:T(8,128)}, f32[256,256]{1,0:T(8,128)}, bf16[256,128]{1,0:T(8,128)(2,1)}, bf16[256,128]{1,0:T(8,128)(2,1)}, bf16[32,3,2,8,128]{4,3,...) custom-call(bf16[256,1024]{1,0:T(8,128)(2,1)} %tok_ref.1, f32[1,1024]{1,0:T(1,128)} %bitcast.13, ...), custom_call_target="tpu_custom_call" | custom-call | tf_op jit(solution)/shard_map/gather/pallas_call | solution.py:571
  205.9 0.0 copy-start
  205.9 6.0 %attend.1 = bf16[256,512]{1,0:T(8,128)(2,1)} custom-call(f32[256,256]{1,0:T(8,128)} %get-tuple-element.8.q0_ref, f32[256,256]{1,0:T(8,128)} %get-tuple-element.9.q1_ref, f32[1,512]{1,0:T(1,128)} %bitcast.15, f32[384,128]{1,0:T(8,128)} %get-tuple-element.17.cos_ref, f32[384,128]{1,0:T(8,128)} %get-tuple-element.18.sin_ref, ...), custom_call_target="tpu_custom_call" | custom-call | tf_op jit(solution)/shard_map/attend/pallas_call | solution.py:627
  211.9 0.0 copy-done
  211.9 0.7 copy.14
  (1 shorter events, 0.0 us)
Async XLA Ops:
  0.6 0.7 copy-start.1
  205.9 6.0 %copy-start = (bf16[32,2,2,8,128]{4,3,2,1,0:T(8,128)(2,1)S(1)}, bf16[32,2,2,8,128]{4,3,2,1,0:T(8,128)(2,1)}, u32[]{:S(2)}) copy-start(bf16[32,2,2,8,128]{4,3,2,1,0:T(8,128)(2,1)} %get-tuple-element.13) | copy-start | bytes 786436

commit v3 on v2

--- a/solution.py
+++ b/solution.py
@@ -3,6 +3,7 @@
 
 import jax
 import jax.numpy as jnp
+import numpy as np
 from jax import lax
 from jax.experimental import pallas as pl
 from jax.experimental.pallas import tpu as pltpu
@@ -13,9 +14,9 @@
 PAGE = 8
 MESH = pl.DeviceIdType.MESH
 
-PREFIX_LAG = 6
-Z_LAG = (0, 1, 3)
-Y_WAIT = (0, 0, 8)
+PREFIX_LAG = 4
+Z_LAG = (0, 2)
+Y_WAIT = (0, 3)
 GROUPS_AT_ONCE = 2
 
 
@@ -54,8 +55,8 @@
     n_parts, n_seq, n_tp,
     tok_ref, gain_ref, wkv_ref, wq_ref, bkv_ref, cos_ref, sin_ref, pool_ref,
     pages_ref, plen_ref, slen_ref, owner_ref,
-    q0_ref, q1_ref, knew_ref, vnew_ref, got_ref, fresh_ref,
-    toks, gains, nrm, wkvb, wqb0, wqb1, acc, psend, pg_r, pg_l, fsend, fgot, newp, source,
+    q_ref, knew_ref, vnew_ref, got_ref, fresh_ref,
+    toks, gains, nrm, wkvb, wqb, acc, psend, pg_r, pg_l, fsend, fgot, newp, source,
     ring_send, ring_recv, y_send, y_recv, tok_send, tok_recv, gain_send, gain_recv,
     fresh_send, fresh_recv,
 ):
@@ -71,7 +72,6 @@
     rows, features = tok_ref.shape
     half = rows // 2
     depth = wkv_ref.shape[0] * wkv_ref.shape[1]
-    q_cols = q0_ref.shape[1]
     pool_pages = pool_ref.shape[0]
     requests = rows // BLOCK
     fresh_entries = rows // PAGE
@@ -116,11 +116,10 @@
 
         return Ring(make, n_r if direction == 0 else n_l)
 
-    buffers = (wkvb, wqb0, wqb1)
+    buffers = (wkvb, wqb)
     owns = (
         lambda: wkv_ref.at[part],
-        lambda: wq_ref.at[part, :, pl.ds(0, q_cols)],
-        lambda: wq_ref.at[part, :, pl.ds(q_cols, q_cols)],
+        lambda: wq_ref.at[part],
     )
 
     def weight_refs(which, direction):
@@ -148,8 +147,8 @@
 
         return refs
 
-    weights = [[ring(w, d, weight_refs(w, d)) for d in (0, 1)] for w in range(3)]
-    prefix = [ring(3, d, prefix_refs(d)) for d in (0, 1)]
+    weights = [[ring(w, d, weight_refs(w, d)) for d in (0, 1)] for w in range(2)]
+    prefix = [ring(2, d, prefix_refs(d)) for d in (0, 1)]
 
     y_open = {}
 
@@ -208,8 +207,7 @@
     toks[tp] = tok_ref[...]
     gains[tp] = gain_ref[...]
     acc[...] = jnp.zeros_like(acc)
-    q0_ref[...] = jnp.zeros_like(q0_ref)
-    q1_ref[...] = jnp.zeros_like(q1_ref)
+    q_ref[...] = jnp.zeros_like(q_ref)
 
     def tokens_near():
         tok_copy(1, None, x_left, None, x_right).wait_recv()
@@ -267,13 +265,13 @@
             nrm[shard], weight.reshape(depth, -1), preferred_element_type=jnp.float32
         )
 
-    sums = (acc, q0_ref, q1_ref)
-    done = [0, 0, 0]
+    sums = (acc, q_ref)
+    done = [0, 0]
 
     def product(which, step):
         done[which] += 1
         if step == 0:
-            own = wkv_ref[...] if which == 0 else wq_ref[:, :, (which - 1) * q_cols : which * q_cols]
+            own = (wkv_ref, wq_ref)[which][...]
             sums[which][...] += dot(me, own)
             return
         total = dot(origin(0, step), buffers[which][2 * step - 1])
@@ -388,7 +386,7 @@
     ready = 7
     for it in range(1, last + 1):
         busy = compute if it > ready else fill
-        for w in range(3):
+        for w in range(2):
             step = it - Z_LAG[w]
             if step == 0:
                 for d in (0, 1):
@@ -401,7 +399,7 @@
             if 1 <= step <= n_r:
                 for d in (0, 1):
                     y_start(w, step, d, 1)
-            busy(1)
+            busy(2)
         step = it - PREFIX_LAG
         if step == 0:
             fill(len(work))
@@ -417,7 +415,7 @@
             if step <= n_l:
                 got_ref[2 * step] = pg_l[starts[1][step - 1]]
         busy(1)
-        for w in range(3):
+        for w in range(2):
             for hop in range(1, y_max + 1):
                 step = it - Z_LAG[w] - Y_WAIT[w] - hop - 1
                 if 1 <= step <= n_r:
@@ -448,7 +446,7 @@
                 copy.start()
                 opened.append(copy)
     compute(len(products))
-    assert done == [n_r + 1] * 3 and not work
+    assert done == [n_r + 1] * 2 and not work
 
     for d, step in far_first:
         fresh_copy(d, step, True).wait_recv()
@@ -462,16 +460,16 @@
 
 def attend_kernel(
     n_seq, pool_pages,
-    q0_ref, q1_ref, bq_ref, cos_ref, sin_ref, knew_ref, vnew_ref, got_ref,
+    q_ref, bq_ref, cos_ref, sin_ref, knew_ref, vnew_ref, got_ref,
     pages_ref, plen_ref, slen_ref,
     out_ref, kall, vall, counts,
 ):
     me = lax.axis_index("seq")
-    rows = q0_ref.shape[0]
+    rows = q_ref.shape[0]
     requests = rows // BLOCK
     slots = pages_ref.shape[0]
     old = slots * PAGE
-    per = q0_ref.shape[1] // HEAD_DIM
+    heads = q_ref.shape[1] // HEAD_DIM
     cap = got_ref.shape[0] // n_seq
     n_r = n_seq // 2
 
@@ -513,8 +511,8 @@
         live = lax.broadcasted_iota(jnp.int32, (BLOCK, HEAD_DIM), 0) < slen_ref[here]
         at = pl.ds(plen_ref[here], BLOCK)
         cos, sin = cos_ref[at, :], sin_ref[at, :]
-        for h in range(2 * per):
-            lin = (q0_ref, q1_ref)[h // per][mine, (h % per) * HEAD_DIM : (h % per + 1) * HEAD_DIM]
+        for h in range(heads):
+            lin = q_ref[mine, h * HEAD_DIM : (h + 1) * HEAD_DIM]
             lin = lin + bq_ref[:, h * HEAD_DIM : (h + 1) * HEAD_DIM]
             query = (lin * cos + pltpu.roll(lin, HEAD_DIM // 2, 1) * sin).astype(jnp.bfloat16)
             scores = lax.dot_general(
@@ -549,17 +547,16 @@
     n_r, n_l = n_seq // 2, (n_seq - 1) // 2
 
     half_dim = HEAD_DIM // 2
-    positions = jnp.arange(slots * PAGE + BLOCK, dtype=jnp.float32)[:, None]
-    inverse = jnp.exp(
-        jnp.arange(half_dim, dtype=jnp.float32) * (-2.0 * math.log(1000000.0) / HEAD_DIM)
+    positions = np.arange(slots * PAGE + BLOCK, dtype=np.float32)[:, None]
+    inverse = np.exp(
+        np.arange(half_dim, dtype=np.float32) * np.float32(-2.0 * math.log(1000000.0) / HEAD_DIM)
     )
     angles = positions * inverse
-    cosine, sine = jnp.cos(angles), jnp.sin(angles)
-    cos_all = jnp.concatenate([cosine, cosine], axis=1)
-    sin_all = jnp.concatenate([-sine, sine], axis=1)
+    cosine, sine = np.cos(angles), np.sin(angles)
+    cos_all = jnp.asarray(np.concatenate([cosine, cosine], axis=1), jnp.float32)
+    sin_all = jnp.asarray(np.concatenate([-sine, sine], axis=1), jnp.float32)
     pages_by_slot = prefix_pages.T
 
-    q_cols = query_width // 2
     piece = depth // n_parts
     y_lanes = max(1, n_parts - 1)
     tri_r, tri_l = offsets(n_r)[1], offsets(n_l)[1]
@@ -568,26 +565,24 @@
     vmem = pl.BlockSpec(memory_space=pltpu.VMEM)
     smem = pl.BlockSpec(memory_space=pltpu.SMEM)
     dma = pltpu.SemaphoreType.DMA
-    q0, q1, knew, vnew, got, fresh = pl.pallas_call(
+    q_sums, knew, vnew, got, fresh = pl.pallas_call(
         functools.partial(gather_kernel, n_parts, n_seq, n_tp),
         name="gather",
         out_shape=(
-            jax.ShapeDtypeStruct((rows, q_cols), f32),
-            jax.ShapeDtypeStruct((rows, q_cols), f32),
+            jax.ShapeDtypeStruct((rows, query_width), f32),
             jax.ShapeDtypeStruct((rows, HEAD_DIM), bf16),
             jax.ShapeDtypeStruct((rows, HEAD_DIM), bf16),
             jax.ShapeDtypeStruct((n_seq, prefix_cap, *page), bf16),
             jax.ShapeDtypeStruct((n_seq, fresh_cap, *page), bf16),
         ),
         in_specs=[vmem] * 8 + [smem] * 4,
-        out_specs=(vmem,) * 6,
+        out_specs=(vmem,) * 5,
         scratch_shapes=[
             pltpu.VMEM((n_tp, rows, features), bf16),
             pltpu.VMEM((n_tp, 1, features), f32),
             pltpu.VMEM((n_seq, rows, depth), bf16),
             pltpu.VMEM((n_seq, n_parts, piece, 2 * kv_width), bf16),
-            pltpu.VMEM((n_seq, n_parts, piece, q_cols), bf16),
-            pltpu.VMEM((n_seq, n_parts, piece, q_cols), bf16),
+            pltpu.VMEM((n_seq, n_parts, piece, query_width), bf16),
             pltpu.VMEM((rows, 2 * kv_width), f32),
             pltpu.VMEM((n_seq, prefix_cap, *page), bf16),
             pltpu.VMEM((tri_r, prefix_cap, *page), bf16),
@@ -596,10 +591,10 @@
             pltpu.VMEM((n_seq, fresh_cap, *page), bf16),
             pltpu.VMEM((fresh_entries + 1, *page), bf16),
             pltpu.SMEM((n_seq * fresh_cap,), jnp.int32),
-            dma((4, 2, 2)),
-            dma((4, 2, n_r)),
-            dma((3, y_lanes, 2)),
-            dma((3, y_lanes, n_r)),
+            dma((3, 2, 2)),
+            dma((3, 2, n_r)),
+            dma((2, y_lanes, 2)),
+            dma((2, y_lanes, n_r)),
             dma((9,)),
             dma((9,)),
             dma((n_tp - 1,)),
@@ -628,7 +623,7 @@
         functools.partial(attend_kernel, n_seq, pool_pages),
         name="attend",
         out_shape=jax.ShapeDtypeStruct((rows, query_width), bf16),
-        in_specs=[vmem] * 8 + [smem] * 3,
+        in_specs=[vmem] * 7 + [smem] * 3,
         out_specs=vmem,
         scratch_shapes=[
             pltpu.VMEM((requests, slots * PAGE + BLOCK, HEAD_DIM), f32),
@@ -636,8 +631,7 @@
             pltpu.SMEM((n_seq,), jnp.int32),
         ],
     )(
-        q0,
-        q1,
+        q_sums,
         b_query.reshape(1, query_width),
         cos_all,
         sin_all,

time: 214 us -> 211 us (0.986)
  no operation moved by 1% of the time
where the time goes in v3:
time: 211 us
  Pallas kernels  206 us (98%)
  local copies, waits for them, and re-layouts  3.03 us (1%)
    pallas_call x1, Pallas kernels, body(): pl.pallas_call(functools.partial(gather_kernel, n_parts, n_seq, n_tp), na...  200 us
    pallas_call x1, Pallas kernels, body(): pl.pallas_call(functools.partial(attend_kernel, n_seq, pool_pages), name=...  6.01 us

profile of v3, /device:TPU:40, one launch (start us, length us, event | category | flops | bytes accessed | tf_op | source)
XLA Modules:
  0.0 210.6 jit_solution(13358693820779990499)
XLA Ops:
  0.6 0.0 copy-start.1
  0.6 0.7 copy-done.1
  1.3 0.6 reshape.39
  1.9 1.6 reshape.32.wkv_ref
  3.6 200.4 %gather.1 = (f32[256,512]{1,0:T(8,128)}, bf16[256,128]{1,0:T(8,128)(2,1)}, bf16[256,128]{1,0:T(8,128)(2,1)}, bf16[32,3,2,8,128]{4,3,2,1,0:T(8,128)(2,1)}, bf16[32,2,2,8,128]{4,3,2,1,0:T(8,128)(2,1)}) custom-call(bf16[256,1024]{1,0:T(8,128)(2,1)} %tok_ref.1, f32[1,1024]{1,0:T(1,128)} %bitcast.13, bf16[2,128,256]{2,1,0:T(8,128)(2,1)} %reshape.32.wkv_ref, ...), custom_call_target="tpu_custom_call" | custom-call | tf_op jit(solution)/shard_map/gather/pallas_call | solution.py:568
  203.9 0.0 copy-start
  203.9 6.0 %attend.1 = bf16[256,512]{1,0:T(8,128)(2,1)} custom-call(f32[256,512]{1,0:T(8,128)} %get-tuple-element.7.q_ref, f32[1,512]{1,0:T(1,128)} %bitcast.15, f32[384,128]{1,0:T(8,128)} %constant.4.clone.cos_ref, f32[384,128]{1,0:T(8,128)} %constant.5.clone.sin_ref, bf16[256,128]{1,0:T(8,128)(2,1)} %get-tuple-element.8.knew_ref, ...), custom_call_target="tpu_custom_call" | custom-call | tf_op jit(solution)/shard_map/attend/pallas_call | solution.py:622
  209.9 0.0 copy-done
  209.9 0.7 copy.16
Async XLA Ops:
  0.6 0.7 copy-start.1
  203.9 6.0 %copy-start = (bf16[32,2,2,8,128]{4,3,2,1,0:T(8,128)(2,1)S(1)}, bf16[32,2,2,8,128]{4,3,2,1,0:T(8,128)(2,1)}, u32[]{:S(2)}) copy-start(bf16[32,2,2,8,128]{4,3,2,1,0:T(8,128)(2,1)} %get-tuple-element.11) | copy-start | bytes 786436
